TPU v7x, 32 devices: a whole 2x2x4 slice. The times are simulated.
32 devices in a mesh: gx: 4 (over y, core), gy: 4 (over z), gz: 2 (over x).
Axes of the slice: x: 2, y: 2, z: 4, core: 2. Of those that a mesh axis runs over, the one named last changes fastest.
Arguments:
- tokens: bfloat16 [256, 7168], P(('gx', 'gy', 'gz')), may hold values from -6 to 6
- expert_ids: int32 [256, 8], P(('gx', 'gy', 'gz')), may hold values from 0 to 15, as said below
- slot_ids: int32 [256, 8], P(('gx', 'gy', 'gz')), may hold values from 0 to 7, as said below
- route_weight: bfloat16 [256, 8], P(('gx', 'gy', 'gz')), may hold values from 0.099609375 to 0.59765625
- gate_weight: bfloat16 [16, 7168, 2048], P(('gx', 'gy'), None, 'gz'), may hold values from -0.0625 to 0.0625
- up_weight: bfloat16 [16, 7168, 2048], P(('gx', 'gy'), None, 'gz'), may hold values from -0.0625 to 0.0625
- down_weight: bfloat16 [16, 2048, 7168], P(('gx', 'gy'), 'gz'), may hold values from -0.125 to 0.125
- expert_bias: float32 [16], replicated, may hold values from -3 to 3
Outputs:
- combined: bfloat16 [256, 7168], P(('gx', 'gy', 'gz'))
- expert_load: int32 [16], replicated
- new_bias: float32 [16], replicated
Inputs may be any that keep to these rules, and one draw needn't show every extreme that they name: `expert_ids`: the 8 experts of a token are different. Among the 8 tokens of one device no expert is named more than 8 times; one expert is named by every token of every device. `slot_ids`: for each device and expert, the routes of that device's tokens to that expert hold different slots.
All inputs are finite; a program needn't handle non-finite values.
Results may differ from a plain program's by a relative error of at most 0.015.
Values may be sent and summed in bfloat16 or wider, within the bound.
A program may use at most 128 MiB of HBM per device.

v0:
```python
import jax
import jax.numpy as jnp
from jax import lax
from jax.sharding import PartitionSpec as P

PLACE_LIMIT = 8


bias_rate = 0.001


def pack_rows(targets, tokens, row_total):
    selection = jnp.any(
        targets[None, :, :] == jnp.arange(row_total, dtype=jnp.int32)[:, None, None], axis=2
    )
    return jnp.dot(
        selection.astype(jnp.bfloat16), tokens, preferred_element_type=jnp.float32
    ).astype(jnp.bfloat16)


def send_rows(buffer):
    arrived = lax.all_to_all(buffer, ("gx", "gy", "gz"), split_axis=1, concat_axis=1, tiled=True)
    return arrived


def return_rows(buffer):
    arrived = lax.all_to_all(buffer, ("gx", "gy", "gz"), split_axis=1, concat_axis=1, tiled=True)
    return arrived


def body(
    tokens, expert_ids, slot_ids, route_weight, gate_weight, up_weight, down_weight, expert_bias
):
    experts = lax.axis_size("gx") * lax.axis_size("gy")
    gz_parts = lax.axis_size("gz")
    devices = experts * gz_parts
    tok_rows, model_width = tokens.shape
    route_count = expert_ids.shape[1]
    capacity = PLACE_LIMIT
    slot_share = capacity // gz_parts
    expert_index = jnp.arange(experts, dtype=jnp.int32)
    local_hits = jnp.sum((expert_ids[:, :, None] == expert_index).astype(jnp.int32), axis=(0, 1))
    expert_load = lax.psum(local_hits, ("gx", "gy", "gz"))
    mean_load = tok_rows * devices * route_count // experts
    new_bias = expert_bias + bias_rate * jnp.sign((mean_load - expert_load).astype(jnp.float32))
    back_rows = slot_ids % slot_share * devices + expert_ids * gz_parts + slot_ids // slot_share
    packed = pack_rows(slot_ids * experts + expert_ids, tokens, capacity * experts)
    repeated = jnp.broadcast_to(
        packed.reshape(capacity, experts, 1, model_width),
        (capacity, experts, gz_parts, model_width),
    )
    received = send_rows(repeated.reshape(capacity, devices, model_width))
    gate_mat = gate_weight[0]
    up_mat = up_weight[0]
    down_mat = down_weight[0]
    flat_rows = received.reshape(slot_share * lax.axis_size("gz") * devices, model_width)
    gate_act = jnp.dot(flat_rows, gate_mat, preferred_element_type=jnp.float32)
    up_act = jnp.dot(flat_rows, up_mat, preferred_element_type=jnp.float32)
    hidden = (jax.nn.silu(gate_act) * up_act).astype(jnp.bfloat16)
    partial_out = jnp.dot(hidden, down_mat, preferred_element_type=jnp.float32)
    summed = lax.psum_scatter(
        partial_out.reshape(slot_share * lax.axis_size("gz"), devices, model_width).astype(
            jnp.bfloat16
        ),
        "gz",
        scatter_dimension=0,
        tiled=True,
    )
    answers = return_rows(summed)
    flat_answers = answers.reshape(slot_share * devices, model_width)
    spread = jnp.where(
        back_rows[:, :, None] == jnp.arange(slot_share * devices, dtype=jnp.int32),
        route_weight.astype(jnp.float32)[:, :, None],
        0.0,
    )
    mixing = jnp.sum(spread, axis=1).astype(jnp.bfloat16)
    combined = jnp.dot(mixing, flat_answers, preferred_element_type=jnp.float32).astype(
        jnp.bfloat16
    )
    return (combined, expert_load, new_bias)


def solution(mesh):
    return jax.shard_map(
        body,
        mesh=mesh,
        in_specs=(
            P(("gx", "gy", "gz"), None),
            P(("gx", "gy", "gz"), None),
            P(("gx", "gy", "gz"), None),
            P(("gx", "gy", "gz"), None),
            P(("gx", "gy"), None, "gz"),
            P(("gx", "gy"), None, "gz"),
            P(("gx", "gy"), "gz", None),
            P(),
        ),
        out_specs=(P(("gx", "gy", "gz"), None), P(), P()),
        check_vma=False,
    )
```

profile of v0, /device:TPU:0, one launch (start us, length us, event | category | flops | bytes accessed | tf_op | source)
XLA Modules:
  0.0 253.8 jit_solution(9949804390127732930)
XLA Ops:
  7.2 0.0 copy-start
  7.2 0.0 reduce-scatter.2.cloned.1.call-start
  7.2 0.7 fusion.18
  7.9 0.1 fusion.15
  8.0 0.0 copy-done
  8.1 0.7 convolution_convert_fusion
  8.8 1.0 copy.17
  9.8 0.4 broadcast_in_dim.29
  10.2 0.0 copy-start.4
  10.2 90.8 %all_to_all.10 = bf16[8,32,7168]{2,0,1:T(8,128)(2,1)S(1)} all-to-all(bf16[8,32,7168]{2,0,1:T(8,128)(2,1)S(1)} %bitcast.28), channel_id=1, replica_groups=mesh['gx'=4,'gy'=4,'gz'=2] {'gx','gy','gz'}, dimensions={1} | all-to-all | bytes 7340032 | tf_op jit(solution)/shard_map/all_to_all | solution.py:22
  101.0 2.0 copy.18
  103.0 0.0 copy-done.4
  103.0 4.1 %fusion.4 = f32[256,1024]{1,0:T(8,128)S(1)} fusion(bf16[256,7168]{1,0:T(8,128)(2,1)S(1)} %bitcast.31, bf16[1,7168,1024]{2,1,0:T(8,128)(2,1)S(1)} %copy-done.4), kind=kOutput, calls=%fused_computation.4 | convolution fusion | flops 3758096384 | bytes 19398656 | tf_op jit(solution)/shard_map/dot_general | solution.py:57
  107.1 7.6 %fusion.12 = bf16[256,1024]{1,0:T(8,128)(2,1)S(1)} fusion(bf16[256,7168]{1,0:T(8,128)(2,1)S(1)} %bitcast.32, bf16[1,7168,1024]{2,1,0:T(8,128)(2,1)} %param.13, f32[256,1024]{1,0:T(8,128)S(1)} %fusion.4), kind=kOutput, calls=%fused_computation.10 | convolution fusion | flops 3759669248 | bytes 19922944 | tf_op jit(solution)/shard_map/dot_general | solution.py:58
  114.7 10.6 %fusion.6 = bf16[8,32,7168]{2,1,0:T(8,128)(2,1)} fusion(bf16[8,32,1024]{2,1,0:T(8,128)(2,1)S(1)} %bitcast.33, bf16[1,1024,7168]{2,1,0:T(8,128)(2,1)} %param.14), kind=kOutput, calls=%fused_computation.6 | convolution fusion | flops 3759931392 | bytes 18874368 | tf_op jit(solution)/shard_map/dot_general | solution.py:60
  125.3 0.0 reduce-scatter.2.cloned.1.call-update
  125.3 0.0 copy-start.2
  125.4 0.0 copy-start.3
  125.4 0.0 copy-start.5
  125.4 47.0 %reduce-scatter.2.cloned.1.call-done = bf16[4,32,7168]{2,1,0:T(8,128)(2,1)} async-done(((bf16[8,32,7168]{2,1,0:T(8,128)(2,1)}), bf16[4,32,7168]{2,1,0:T(8,128)(2,1)}) %reduce-scatter.2.cloned.1.call-update) | async-done | bytes 1835024 | tf_op jit(solution)/shard_map/reduce_scatter | solution.py:61
  172.4 4.2 %copy.19 = bf16[4,32,7168]{2,0,1:T(4,128)(2,1)} copy(bf16[4,32,7168]{2,1,0:T(8,128)(2,1)} %reduce-scatter.2.cloned.1.call-done) | data formatting | bytes 3670016 | tf_op jit(solution)/shard_map/reduce_scatter | solution.py:61
  176.6 4.6 %all-to-all-start.1 = ((bf16[4,32,7168]{2,0,1:T(4,128)(2,1)}), bf16[4,32,7168]{2,0,1:T(4,128)(2,1)S(1)}, u32[]{:S(2)}, u32[]{:S(2)}) async-start(bf16[4,32,7168]{2,0,1:T(4,128)(2,1)} %copy.19), calls=%async_computation.2 | async-start | bytes 3670016 | tf_op jit(solution)/shard_map/all_to_all | solution.py:27
  181.2 0.0 copy-done.2
  181.2 0.0 copy-start.1
  181.2 0.1 convert_reduce_fusion
  181.3 63.4 %psum.7 = s32[16]{0:T(128)S(1)} all-reduce(s32[16]{0:T(128)S(1)} %convert_reduce_fusion), channel_id=1, replica_groups=mesh['gx'=4,'gy'=4,'gz'=2] {'gx','gy','gz'}, use_global_device_ids=true, to_apply=%region_4.5 | all-reduce | flops 16 | bytes 128 | tf_op jit(solution)/shard_map/psum | solution.py:43
  244.7 0.0 copy-done.3
  244.7 0.0 copy-start.6
  244.7 0.1 select_reduce_fusion
  244.8 0.0 copy-done.5
  244.8 0.5 multiply_add_fusion.1
  245.4 0.0 all-to-all-done.1
  245.4 0.5 copy.20
  245.9 1.0 convolution_convert_fusion.1
  246.9 0.0 copy-done.6
  246.9 0.0 copy-done.1
  (1 shorter events, 0.0 us)
Async XLA Ops:
  7.2 0.9 copy-start
  7.2 165.2 %reduce-scatter.2.cloned.1.call-start = ((), (), s32[]{:S(2)}) async-start(), calls=%async_computation.3 | async-start | bytes 5505024 | tf_op jit(solution)/shard_map/reduce_scatter | solution.py:61
  10.2 92.8 %copy-start.4 = (bf16[1,7168,1024]{2,1,0:T(8,128)(2,1)S(1)}, bf16[1,7168,1024]{2,1,0:T(8,128)(2,1)}, u32[]{:S(2)}) copy-start(bf16[1,7168,1024]{2,1,0:T(8,128)(2,1)} %param.12) | copy-start | bytes 44040196
  125.3 55.9 %copy-start.2 = (s32[8,8]{1,0:T(8,128)S(1)}, s32[8,8]{1,0:T(8,128)}, u32[]{:S(2)}) copy-start(s32[8,8]{1,0:T(8,128)} %param.9) | copy-start | bytes 772
  125.4 119.4 %copy-start.3 = (bf16[8,8]{1,0:T(8,128)(2,1)S(1)}, bf16[8,8]{1,0:T(8,128)(2,1)}, u32[]{:S(2)}) copy-start(bf16[8,8]{1,0:T(8,128)(2,1)} %param.11) | copy-start | bytes 388
  125.4 119.5 %copy-start.5 = (f32[16]{0:T(128)S(1)}, f32[16]{0:T(128)}, u32[]{:S(2)}) copy-start(f32[16]{0:T(128)} %param.15) | copy-start | bytes 196
  176.6 68.8 %all-to-all-start.1 = ((bf16[4,32,7168]{2,0,1:T(4,128)(2,1)}), bf16[4,32,7168]{2,0,1:T(4,128)(2,1)S(1)}, u32[]{:S(2)}, u32[]{:S(2)}) async-start(bf16[4,32,7168]{2,0,1:T(4,128)(2,1)} %copy.19), calls=%async_computation.2 | async-start | bytes 3670016 | tf_op jit(solution)/shard_map/all_to_all | solution.py:27
  181.2 65.7 %copy-start.1 = (bf16[8,7168]{1,0:T(8,128)(2,1)S(1)}, bf16[8,7168]{1,0:T(8,128)(2,1)}, u32[]{:S(2)}) copy-start(bf16[8,7168]{1,0:T(8,128)(2,1)} %param.8) | copy-start | bytes 344068
  244.7 2.2 copy-start.6
Sparse Core Ops, SparseCore 0:
  125.5 46.9 reduce-scatter.1
where the time goes:
time: 254 us
  blocking collectives  154 us (61%)
  waiting for transfers between devices  47.1 us (19%)
  matrix products  24 us (9%)
  between operations  14.2 us (6%)
  local copies, waits for them, and re-layouts  8.22 us (3%)
  starting transfers between devices  4.65 us (2%)
    all_to_all x1, blocking collectives, send_rows(): lax.all_to_all(buffer, ('gx', 'gy', 'gz'), split_axis=1, concat_axis=1, t...  90.8 us
    psum x1, blocking collectives, body(): expert_load = lax.psum(local_hits, ('gx', 'gy', 'gz'))  63.4 us
    reduce_scatter x1, waiting for transfers between devices, body(): lax.psum_scatter(partial_out.reshape(slot_share * lax.axis_size('gz'), de...  47 us
    dot_general x1, matrix products, body(): partial_out = jnp.dot(hidden, down_mat, preferred_element_type=jnp.float32)  10.6 us
    dot_general x1, matrix products, body(): up_act = jnp.dot(flat_rows, up_mat, preferred_element_type=jnp.float32)  7.61 us
  transfers between devices with their start and end apart: 2, of which 1 were waited for; matrix products, arithmetic and copies ran while one was open for 0% of the time, Pallas kernels for 0%

commit v1 on v0

--- a/solution.py
+++ b/solution.py
@@ -1,6 +1,8 @@
 import jax
 import jax.numpy as jnp
 from jax import lax
+from jax.experimental import pallas as pl
+from jax.experimental.pallas import tpu as pltpu
 from jax.sharding import PartitionSpec as P
 
 PLACE_LIMIT = 8
@@ -28,7 +30,7 @@
     return arrived
 
 
-def body(
+def slot_body(
     tokens, expert_ids, slot_ids, route_weight, gate_weight, up_weight, down_weight, expert_bias
 ):
     experts = lax.axis_size("gx") * lax.axis_size("gy")
@@ -80,6 +82,395 @@
     return (combined, expert_load, new_bias)
 
 
+PAIR = 1024
+HALF = PAIR // 2
+TILE = 256
+LANES = 128
+MESH = pl.DeviceIdType.MESH
+
+
+def layer_kernel(
+    tok_ref, ids_ref, rw_ref, wg_hbm, wu_hbm, wd_hbm,
+    out_ref, cnt_ref,
+    wg, wu, wd, gath, meta, xbuf, acc_g, acc_u, hid,
+    s0, r1, s1, r2, s2, r3, s3, r4,
+    w_sem, gz_s, gz_r, g1_s, g1_r, g2_s, g2_r, g3_s, g3_r,
+    c1_s, c1_r, c2_s, c2_r, c3_s, c3_r, c4_s, c4_r,
+):
+    f32, bf16 = jnp.float32, jnp.bfloat16
+    gx, z, x = lax.axis_index("gx"), lax.axis_index("gy"), lax.axis_index("gz")
+    nz = lax.axis_size("gy")
+    experts = lax.axis_size("gx") * nz
+    y, core = gx // 2, gx % 2
+    rows = tok_ref.shape[0]
+    total = gath.shape[1] * gath.shape[2] * gath.shape[3] * nz * rows
+    ff = hid.shape[1]
+    pairs = gath.shape[0] // 2
+    sib = (y * 2 + (1 - core), z, x)
+    ypeer = ((1 - y) * 2 + core, z, x)
+    xpeer = (gx, z, 1 - x)
+
+    def zpeer(d):
+        return (gx, lax.rem(z + d, nz), x)
+
+    def wcopies(j):
+        span = pl.ds(pl.multiple_of(j * PAIR, PAIR), PAIR)
+        return (
+            pltpu.make_async_copy(wg_hbm.at[0, span, :], wg.at[j], w_sem.at[0, j]),
+            pltpu.make_async_copy(wu_hbm.at[0, span, :], wu.at[j], w_sem.at[1, j]),
+        )
+
+    def dcopy(j):
+        span = pl.ds(pl.multiple_of(j * PAIR, PAIR), PAIR)
+        return pltpu.make_async_copy(wd_hbm.at[0, :, span], wd.at[j], w_sem.at[2, j])
+
+    def start_gate(j, carry):
+        for c in wcopies(j):
+            c.start()
+        return carry
+
+    def start_down(j, carry):
+        dcopy(j).start()
+        return carry
+
+    lax.fori_loop(0, pairs, start_gate, 0)
+    lax.fori_loop(0, pairs, start_down, 0)
+
+    ids = ids_ref[...]
+    rw = rw_ref[...].astype(f32)
+    lane = lax.broadcasted_iota(jnp.int32, (rows, LANES), 1)
+    table = jnp.zeros((rows, LANES), f32)
+    for k in range(ids.shape[1]):
+        col = ids[:, k:k + 1]
+        table = table + jnp.where(lane == col, rw[:, k:k + 1], 0.0)
+        table = table + jnp.where(lane == col + experts, 1.0, 0.0)
+    meta[core, y, x, z] = table.astype(bf16)
+
+    barrier = pltpu.get_barrier_semaphore()
+    peers = [sib, ypeer, xpeer] + [zpeer(d) for d in range(1, nz)]
+    for peer in peers:
+        pl.semaphore_signal(barrier, inc=1, device_id=peer, device_id_type=MESH)
+    pl.semaphore_wait(barrier, len(peers))
+
+    def remote(src, dst, ssem, rsem, dev):
+        return pltpu.make_async_remote_copy(
+            src_ref=src, dst_ref=dst, send_sem=ssem, recv_sem=rsem,
+            device_id=dev, device_id_type=MESH,
+        )
+
+    last = pairs * 2
+
+    def view(q):
+        return meta if q is None else gath.at[q]
+
+    def semi(q):
+        return last if q is None else q
+
+    def cols(q):
+        return pl.ds(pl.multiple_of(q * HALF, HALF), HALF)
+
+    def gz(q, d, inn=False):
+        buf = view(q)
+        own = buf.at[core, y, x, z]
+        src = meta.at[core, y, x, z] if q is None else tok_ref.at[:, cols(q)]
+        dst = buf.at[core, y, x, lax.rem(z - d + nz, nz)] if inn else own
+        return remote(src, dst, gz_s.at[semi(q), d - 1], gz_r.at[semi(q), d - 1], zpeer(d))
+
+    def own_copy(q):
+        return pltpu.make_async_copy(
+            tok_ref.at[:, cols(q)], gath.at[q, core, y, x, z], w_sem.at[3, q]
+        )
+
+    def g1(q, par, inn=False):
+        buf = view(q)
+        src = buf.at[core, y, x]
+        if par == 0:
+            dst = buf.at[core, y, 1 - x] if inn else src
+            dev = xpeer
+        else:
+            dst = buf.at[core, 1 - y, x] if inn else src
+            dev = ypeer
+        return remote(src, dst, g1_s.at[semi(q)], g1_r.at[semi(q)], dev)
+
+    def g2(q, par, inn=False):
+        buf = view(q)
+        if par == 0:
+            src = buf.at[core, y]
+            dst = buf.at[core, 1 - y] if inn else src
+            dev = ypeer
+        else:
+            src = buf.at[core, :, x]
+            dst = buf.at[core, :, 1 - x] if inn else src
+            dev = xpeer
+        return remote(src, dst, g2_s.at[semi(q)], g2_r.at[semi(q)], dev)
+
+    def g3(q, inn=False):
+        buf = view(q)
+        src = buf.at[core]
+        dst = buf.at[1 - core] if inn else src
+        return remote(src, dst, g3_s.at[semi(q)], g3_r.at[semi(q)], sib)
+
+    for d in range(1, nz):
+        gz(None, d).start()
+
+    def send_z(i, carry):
+        for par in (0, 1):
+            q = 2 * i + par
+            for d in range(1, nz):
+                gz(q, d).start()
+            own_copy(q).start()
+        return carry
+
+    lax.fori_loop(0, pairs, send_z, 0)
+
+    for d in range(1, nz):
+        gz(None, d, True).wait_recv()
+    g1(None, 0).start()
+
+    acc_g[...] = jnp.zeros_like(acc_g)
+    acc_u[...] = jnp.zeros_like(acc_u)
+
+    def gather_step(i, carry):
+        @pl.when(i < pairs)
+        def _():
+            for par in (0, 1):
+                q = 2 * i + par
+                own_copy(q).wait()
+                for d in range(1, nz):
+                    gz(q, d, True).wait_recv()
+                g1(q, par).start()
+
+        @pl.when(i == 0)
+        def _():
+            g1(None, 0, True).wait_recv()
+            g2(None, 0).start()
+
+        @pl.when((i >= 1) & (i < pairs + 1))
+        def _():
+            for par in (0, 1):
+                q = 2 * (i - 1) + par
+                g1(q, par, True).wait_recv()
+                g2(q, par).start()
+
+        @pl.when(i == 1)
+        def _():
+            g2(None, 0, True).wait_recv()
+            g3(None).start()
+
+        @pl.when((i >= 2) & (i < pairs + 2))
+        def _():
+            for par in (0, 1):
+                q = 2 * (i - 2) + par
+                g2(q, par, True).wait_recv()
+                g3(q).start()
+
+        @pl.when(i >= 3)
+        def _():
+            j = i - 3
+            for par in (0, 1):
+                q = 2 * j + par
+                g3(q, True).wait_recv()
+                xbuf[:, par * HALF:(par + 1) * HALF] = (
+                    gath[q].astype(f32).reshape(total, HALF).astype(bf16)
+                )
+            for c in wcopies(j):
+                c.wait()
+
+            def tile(n, c2):
+                at = pl.ds(pl.multiple_of(n * TILE, TILE), TILE)
+                acc_g[:, at] += jnp.dot(xbuf[...], wg[j, :, at], preferred_element_type=f32)
+                acc_u[:, at] += jnp.dot(xbuf[...], wu[j, :, at], preferred_element_type=f32)
+                return c2
+
+            lax.fori_loop(0, ff // TILE, tile, 0)
+
+        return carry
+
+    lax.fori_loop(0, pairs + 3, gather_step, 0)
+    g3(None, True).wait_recv()
+
+    full = meta[...].astype(f32).reshape(total, LANES)
+    cnt_ref[...] = jnp.broadcast_to(jnp.sum(full, axis=0, keepdims=True), cnt_ref.shape)
+    mine = gx * nz + z
+    lane2 = lax.broadcasted_iota(jnp.int32, (total, LANES), 1)
+    weight = jnp.sum(jnp.where(lane2 == mine, full, 0.0), axis=1, keepdims=True)
+
+    for n in range(ff // TILE):
+        at = slice(n * TILE, (n + 1) * TILE)
+        g = acc_g[:, at]
+        hid[:, at] = (g / (1.0 + jnp.exp(-g)) * acc_u[:, at] * weight).astype(bf16)
+
+    def c1(q):
+        return remote(s0.at[q, 1 - core], r1.at[q], c1_s.at[q], c1_r.at[q], sib)
+
+    def c2(q, par):
+        if par == 0:
+            src, dev = s1.at[q, 1 - y], ypeer
+        else:
+            src, dev = s1.at[q, :, 1 - x], xpeer
+        return remote(src, r2.at[q], c2_s.at[q], c2_r.at[q], dev)
+
+    def c3(q, par):
+        if par == 0:
+            src, dev = s2.at[q, 1 - x], xpeer
+        else:
+            src, dev = s2.at[q, 1 - y], ypeer
+        return remote(src, r3.at[q], c3_s.at[q], c3_r.at[q], dev)
+
+    def c4(q, d):
+        return remote(
+            s3.at[q, lax.rem(z + d, nz)], r4.at[q, d - 1],
+            c4_s.at[q, d - 1], c4_r.at[q, d - 1], zpeer(d),
+        )
+
+    def add(a, b):
+        return (a.astype(f32) + b.astype(f32)).astype(bf16)
+
+    def reduce_step(i, carry):
+        @pl.when(i < pairs)
+        def _():
+            dcopy(i).wait()
+            for n in range(PAIR // TILE):
+                part = jnp.dot(
+                    hid[...], wd[i, :, n * TILE:(n + 1) * TILE], preferred_element_type=f32
+                )
+                lo = n * TILE % HALF
+                s0[2 * i + n * TILE // HALF, :, :, :, :, :, lo:lo + TILE] = part.reshape(
+                    s0.shape[1:-1] + (TILE,)
+                ).astype(bf16)
+            for par in (0, 1):
+                c1(2 * i + par).start()
+
+        @pl.when((i >= 1) & (i < pairs + 1))
+        def _():
+            for par in (0, 1):
+                q = 2 * (i - 1) + par
+                c1(q).wait_recv()
+                s1[q] = add(s0[q, core], r1[q])
+                c2(q, par).start()
+
+        @pl.when((i >= 2) & (i < pairs + 2))
+        def _():
+            for par in (0, 1):
+                q = 2 * (i - 2) + par
+                c2(q, par).wait_recv()
+                s2[q] = add(s1[q, y] if par == 0 else s1[q, :, x], r2[q])
+                c3(q, par).start()
+
+        @pl.when((i >= 3) & (i < pairs + 3))
+        def _():
+            for par in (0, 1):
+                q = 2 * (i - 3) + par
+                c3(q, par).wait_recv()
+                s3[q] = add(s2[q, x] if par == 0 else s2[q, y], r3[q])
+                for d in range(1, nz):
+                    c4(q, d).start()
+
+        @pl.when(i >= 4)
+        def _():
+            for par in (0, 1):
+                q = 2 * (i - 4) + par
+                done = s3[q, z].astype(f32)
+                for d in range(1, nz):
+                    c4(q, d).wait_recv()
+                    done = done + r4[q, d - 1].astype(f32)
+                out_ref[:, cols(q)] = done.astype(bf16)
+
+        return carry
+
+    lax.fori_loop(0, pairs + 4, reduce_step, 0)
+
+    def drain(i, carry):
+        for par in (0, 1):
+            q = 2 * i + par
+            for d in range(1, nz):
+                gz(q, d).wait_send()
+                c4(q, d).wait_send()
+            g1(q, par).wait_send()
+            g2(q, par).wait_send()
+            g3(q).wait_send()
+            c1(q).wait_send()
+            c2(q, par).wait_send()
+            c3(q, par).wait_send()
+        return carry
+
+    lax.fori_loop(0, pairs, drain, 0)
+    for d in range(1, nz):
+        gz(None, d).wait_send()
+    g1(None, 0).wait_send()
+    g2(None, 0).wait_send()
+    g3(None).wait_send()
+
+
+def fused_body(
+    tokens, expert_ids, slot_ids, route_weight, gate_weight, up_weight, down_weight, expert_bias
+):
+    nz = lax.axis_size("gy")
+    experts = lax.axis_size("gx") * nz
+    devices = experts * lax.axis_size("gz")
+    rows, width = tokens.shape
+    ff = gate_weight.shape[2]
+    total = rows * devices
+    pairs = width // PAIR
+    chunks = 2 * pairs
+    bf16, f32 = jnp.bfloat16, jnp.float32
+    vm = pl.BlockSpec(memory_space=pltpu.VMEM)
+    hbm = pl.BlockSpec(memory_space=pl.ANY)
+    dma = pltpu.SemaphoreType.DMA
+    blk = (nz, rows, HALF)
+    combined, counts = pl.pallas_call(
+        layer_kernel,
+        out_shape=(
+            jax.ShapeDtypeStruct((rows, width), bf16),
+            jax.ShapeDtypeStruct((8, LANES), f32),
+        ),
+        in_specs=[vm, vm, vm, hbm, hbm, hbm],
+        out_specs=(vm, vm),
+        scratch_shapes=[
+            pltpu.VMEM((pairs, PAIR, ff), bf16),
+            pltpu.VMEM((pairs, PAIR, ff), bf16),
+            pltpu.VMEM((pairs, ff, PAIR), bf16),
+            pltpu.VMEM((chunks, 2, 2, 2) + blk, bf16),
+            pltpu.VMEM((2, 2, 2, nz, rows, LANES), bf16),
+            pltpu.VMEM((total, PAIR), bf16),
+            pltpu.VMEM((total, ff), f32),
+            pltpu.VMEM((total, ff), f32),
+            pltpu.VMEM((total, ff), bf16),
+            pltpu.VMEM((chunks, 2, 2, 2) + blk, bf16),
+            pltpu.VMEM((chunks, 2, 2) + blk, bf16),
+            pltpu.VMEM((chunks, 2, 2) + blk, bf16),
+            pltpu.VMEM((chunks, 2) + blk, bf16),
+            pltpu.VMEM((chunks, 2) + blk, bf16),
+            pltpu.VMEM((chunks,) + blk, bf16),
+            pltpu.VMEM((chunks,) + blk, bf16),
+            pltpu.VMEM((chunks, nz - 1, rows, HALF), bf16),
+            dma((4, chunks)),
+            dma((chunks + 1, nz - 1)), dma((chunks + 1, nz - 1)),
+            dma((chunks + 1,)), dma((chunks + 1,)),
+            dma((chunks + 1,)), dma((chunks + 1,)),
+            dma((chunks + 1,)), dma((chunks + 1,)),
+            dma((chunks,)), dma((chunks,)),
+            dma((chunks,)), dma((chunks,)),
+            dma((chunks,)), dma((chunks,)),
+            dma((chunks, nz - 1)), dma((chunks, nz - 1)),
+        ],
+        compiler_params=pltpu.CompilerParams(
+            collective_id=0, has_side_effects=True, vmem_limit_bytes=67043328
+        ),
+        name="expert_layer",
+    )(tokens, expert_ids, route_weight, gate_weight, up_weight, down_weight)
+    expert_load = counts[0, experts:2 * experts].astype(jnp.int32)
+    mean_load = total * expert_ids.shape[1] // experts
+    new_bias = expert_bias + bias_rate * jnp.sign((mean_load - expert_load).astype(f32))
+    return (combined, expert_load, new_bias)
+
+
+def body(tokens, *rest):
+    sizes = (lax.axis_size("gx"), lax.axis_size("gz"))
+    fits = sizes == (4, 2) and tokens.shape[0] == 8 and tokens.shape[1] % PAIR == 0
+    return (fused_body if fits else slot_body)(tokens, *rest)
+
+
 def solution(mesh):
     return jax.shard_map(
         body,

time: 254 us -> 74.7 us (0.29)
  blocking collectives: 154 us -> 0 us
  Pallas kernels: 0 us -> 71 us
  waiting for transfers between devices: 47.1 us -> 0 us
  matrix products: 24 us -> 0 us
  between operations: 14.2 us -> 0.64 us
  local copies, waits for them, and re-layouts: 8.22 us -> 1.55 us
  starting transfers between devices: 4.65 us -> 0 us
    all_to_all x1 -> x0, blocking collectives: 90.8 us -> none  [send_rows(): lax.all_to_all(buffer, ('gx', 'gy', 'gz'), split_axis=1, concat_axis=1, t...]
    pallas_call x0 -> x1, Pallas kernels: none -> 71 us  [fused_body(): pl.pallas_call(layer_kernel, out_shape=(jax.ShapeDtypeStruct((rows, width...]
    psum x1 -> x0, blocking collectives: 63.4 us -> none  [body(): expert_load = lax.psum(local_hits, ('gx', 'gy', 'gz'))]
    reduce_scatter x1 -> x0, waiting for transfers between devices: 47 us -> none  [body(): lax.psum_scatter(partial_out.reshape(slot_share * lax.axis_size('gz'), de...]
    dot_general x5 -> x0, matrix products: 24 us -> none  [the longest x1 10.6 us: body(): partial_out = jnp.dot(hidden, down_mat, preferred_element_type=jnp.float32)]
    all_to_all x1 -> x0, starting transfers between devices: 4.61 us -> none  [return_rows(): lax.all_to_all(buffer, ('gx', 'gy', 'gz'), split_axis=1, concat_axis=1, t...]
    reduce_scatter x1 -> x0, local copies, waits for them, and re-layouts: 4.17 us -> none  [body(): lax.psum_scatter(partial_out.reshape(slot_share * lax.axis_size('gz'), de...]
    all_to_all x2 -> x0, local copies, waits for them, and re-layouts: 2.55 us -> none  [the longest x1 2.01 us: send_rows(): lax.all_to_all(buffer, ('gx', 'gy', 'gz'), split_axis=1, concat_axis=1, t...]
  transfers between devices with their start and end apart: 2 -> 0, of which waited for: 1 -> 0; matrix products, arithmetic and copies ran while one was open for 0% -> 0% of each run, Pallas kernels for 0% -> 0%
where the time goes in v1:
time: 74.7 us; the launch traced here: 74.5 us
  Pallas kernels  71 us (95%)
  local copies, waits for them, and re-layouts  1.55 us (2%)
  other arithmetic  1.3 us (2%)
    pallas_call x1, Pallas kernels, fused_body(): pl.pallas_call(layer_kernel, out_shape=(jax.ShapeDtypeStruct((rows, width...  71 us
    unnamed x1, local copies, waits for them, and re-layouts  1.55 us

profile of v1, /device:TPU:0, one launch (start us, length us, event | category | flops | bytes accessed | tf_op | source)
XLA Modules:
  0.0 74.5 jit_solution(13453229728014038636)
XLA Ops:
  0.6 71.0 %expert_layer.1 = (bf16[8,7168]{1,0:T(8,128)(2,1)}, f32[8,128]{1,0:T(8,128)}) custom-call(bf16[8,7168]{1,0:T(8,128)(2,1)} %tok_ref.1, s32[8,8]{1,0:T(8,128)} %ids_ref.1, bf16[8,8]{1,0:T(8,128)(2,1)} %rw_ref.1, bf16[1,7168,1024]{2,1,0:T(8,128)(2,1)} %wg_hbm.1, bf16[1,7168,1024]{2,1,0:T(8,128)(2,1)} %wu_hbm.1, bf16[1,1024,7168]{2,1,0:T(8,128)(2,1)} %wd_hbm.1), custom_call_target="tpu_custom_call" | custom-call | tf_op jit(solution)/shard_map/expert_layer/pallas_call | solution.py:421
  71.7 1.3 %multiply_add_fusion = (f32[16]{0:T(128)}, s32[16]{0:T(128)}) fusion(f32[16]{0:T(128)} %param.14, f32[8,128]{1,0:T(8,128)} %get-tuple-element.6), kind=kLoop, calls=%fused_computation | loop fusion | flops 96 | bytes 256 | tf_op jit(solution)/shard_map/add | solution.py:464
  73.0 1.6 %copy.11 = bf16[8,7168]{1,0:T(8,128)(2,1)} copy(bf16[8,7168]{1,0:T(8,128)(2,1)} %get-tuple-element.12) | data formatting | bytes 229376

commit v2 on v1

--- a/solution.py
+++ b/solution.py
@@ -82,7 +82,7 @@
     return (combined, expert_load, new_bias)
 
 
-PAIR = 1024
+PAIR = 1792
 HALF = PAIR // 2
 TILE = 256
 LANES = 128
@@ -330,15 +330,11 @@
         @pl.when(i < pairs)
         def _():
             dcopy(i).wait()
-            for n in range(PAIR // TILE):
+            for par in (0, 1):
                 part = jnp.dot(
-                    hid[...], wd[i, :, n * TILE:(n + 1) * TILE], preferred_element_type=f32
+                    hid[...], wd[i, :, par * HALF:(par + 1) * HALF], preferred_element_type=f32
                 )
-                lo = n * TILE % HALF
-                s0[2 * i + n * TILE // HALF, :, :, :, :, :, lo:lo + TILE] = part.reshape(
-                    s0.shape[1:-1] + (TILE,)
-                ).astype(bf16)
-            for par in (0, 1):
+                s0[2 * i + par] = part.reshape(s0.shape[1:-1] + (HALF,)).astype(bf16)
                 c1(2 * i + par).start()
 
         @pl.when((i >= 1) & (i < pairs + 1))

time: 74.7 us -> 69.3 us (0.928)
  Pallas kernels: 71 us -> 65.6 us
    pallas_call x1, Pallas kernels: 71 us -> 65.6 us  [fused_body(): pl.pallas_call(layer_kernel, out_shape=(jax.ShapeDtypeStruct((rows, width...]
where the time goes in v2:
time: 69.3 us; the launch traced here: 69.1 us
  Pallas kernels  65.6 us (95%)
  local copies, waits for them, and re-layouts  1.55 us (2%)
  other arithmetic  1.3 us (2%)
    pallas_call x1, Pallas kernels, fused_body(): pl.pallas_call(layer_kernel, out_shape=(jax.ShapeDtypeStruct((rows, width...  65.6 us
    unnamed x1, local copies, waits for them, and re-layouts  1.55 us

profile of v2, /device:TPU:0, one launch (start us, length us, event | category | flops | bytes accessed | tf_op | source)
XLA Modules:
  0.0 69.1 jit_solution(2782877156147444381)
XLA Ops:
  0.6 65.6 %expert_layer.1 = (bf16[8,7168]{1,0:T(8,128)(2,1)}, f32[8,128]{1,0:T(8,128)}) custom-call(bf16[8,7168]{1,0:T(8,128)(2,1)} %tok_ref.1, s32[8,8]{1,0:T(8,128)} %ids_ref.1, bf16[8,8]{1,0:T(8,128)(2,1)} %rw_ref.1, bf16[1,7168,1024]{2,1,0:T(8,128)(2,1)} %wg_hbm.1, bf16[1,7168,1024]{2,1,0:T(8,128)(2,1)} %wu_hbm.1, bf16[1,1024,7168]{2,1,0:T(8,128)(2,1)} %wd_hbm.1), custom_call_target="tpu_custom_call" | custom-call | tf_op jit(solution)/shard_map/expert_layer/pallas_call | solution.py:417
  66.2 1.3 %multiply_add_fusion = (f32[16]{0:T(128)}, s32[16]{0:T(128)}) fusion(f32[16]{0:T(128)} %param.14, f32[8,128]{1,0:T(8,128)} %get-tuple-element.6), kind=kLoop, calls=%fused_computation | loop fusion | flops 96 | bytes 256 | tf_op jit(solution)/shard_map/add | solution.py:460
  67.5 1.6 %copy.11 = bf16[8,7168]{1,0:T(8,128)(2,1)} copy(bf16[8,7168]{1,0:T(8,128)(2,1)} %get-tuple-element.12) | data formatting | bytes 229376
